TPU v7x, 32 devices: a whole 2x2x4 slice. The times are simulated.
32 devices in a mesh: ga: 2 (over core), band: 16 (over z, y, x).
Axes of the slice: x: 2, y: 2, z: 4, core: 2. Of those that a mesh axis runs over, the one named last changes fastest.
Arguments:
- orbitals: bfloat16 [1024, 2, 16384], P('band', None, 'ga'), may hold values from -6 to 6
- projectors: bfloat16 [864, 2, 16384], P(None, None, ('ga', 'band')), may hold values from -0.03125 to 0.03125
- coupling: float32 [4, 18, 18], replicated, may hold values from -6 to 6
- species: int32 [48], replicated, may hold values from 0 to 3
- offsets: int32 [48], replicated, may hold values from 0 to 846, as said below
Outputs:
- applied: bfloat16 [1024, 2, 16384], P('band', None, 'ga')
Inputs may be any that keep to these rules, and one draw needn't show every extreme that they name: Each atom's 18 projectors are the 18 consecutive rows of projectors starting at its offset; offsets are multiples of 18, and the atoms' blocks are distinct and cover all 864 rows.
All inputs are finite; a program needn't handle non-finite values.
Results may differ from a plain program's by a relative error of at most 0.0049.
Values may be sent and summed in bfloat16 or wider, within the bound.
A program may use at most 64 MiB of HBM per device.

v0:
```python
import jax
import jax.numpy as jnp
from jax import lax
from jax.sharding import PartitionSpec as P


def block_matrices(coupling, species, offsets):
    per_atom = coupling.shape[1]
    count = offsets.shape[0]
    blocks = jnp.arange(count, dtype=jnp.int32)
    matches = (offsets[None, :] == blocks[:, None] * per_atom).astype(jnp.int32)
    atom_kind = jnp.sum(matches * species[None, :], axis=1)
    onehot = (atom_kind[:, None] == jnp.arange(coupling.shape[0], dtype=jnp.int32)[None, :]).astype(
        jnp.float32
    )
    table = coupling.reshape(coupling.shape[0], per_atom * per_atom)
    picked = jnp.dot(
        onehot, table, precision=lax.Precision.HIGHEST, preferred_element_type=jnp.float32
    )
    return picked.reshape(count, per_atom, per_atom)


def apply_coupling(matrices, becp):
    count = matrices.shape[0]
    per_atom = matrices.shape[1]
    height = becp.shape[0]
    widths = becp.shape[2]
    blocked = becp.reshape(count, per_atom, 2 * widths)
    coupled = jnp.einsum("aij,ajc->aic", matrices, blocked, precision=lax.Precision.HIGHEST)
    return coupled.reshape(height, 2, widths).astype(jnp.bfloat16)


def project_bands(projectors, spread):
    total_proj = projectors.shape[0]
    total_bands = spread.shape[0]
    flat_proj = projectors.reshape(total_proj, -1)
    turned = jnp.concatenate([spread[:, 1, :], -spread[:, 0, :]], axis=1)
    stacked = jnp.concatenate([spread.reshape(total_bands, -1), turned], axis=0)
    partial_value = lax.dot_general(
        flat_proj, stacked, (((1,), (1,)), ((), ())), preferred_element_type=jnp.float32
    )
    return partial_value.reshape(total_proj, 2, total_bands)


def add_back(projectors, dbecp):
    total_proj = projectors.shape[0]
    total_bands = dbecp.shape[2]
    columns = dbecp.reshape(total_proj, 2 * total_bands)
    real_part = lax.dot_general(
        columns, projectors[:, 0, :], (((0,), (0,)), ((), ())), preferred_element_type=jnp.float32
    )
    imag_part = lax.dot_general(
        columns, projectors[:, 1, :], (((0,), (0,)), ((), ())), preferred_element_type=jnp.float32
    )
    out_real = real_part[:total_bands] - imag_part[total_bands:]
    out_imag = imag_part[:total_bands] + real_part[total_bands:]
    return jnp.stack([out_real, out_imag], axis=1).astype(jnp.bfloat16)


def per_device(orbitals, projectors, coupling, species, offsets):
    matrices = block_matrices(coupling, species, offsets)
    spread = lax.all_to_all(orbitals, "band", split_axis=2, concat_axis=0, tiled=True)
    partial_value = project_bands(projectors, spread)
    becp = lax.psum(partial_value, ("ga", "band"))
    dbecp = apply_coupling(matrices, becp)
    result = add_back(projectors, dbecp)
    return lax.all_to_all(result, "band", split_axis=0, concat_axis=2, tiled=True)


def solution(mesh):
    placed = (P("band", None, "ga"), P(None, None, ("ga", "band")), P(), P(), P())
    return jax.shard_map(
        per_device, mesh=mesh, in_specs=placed, out_specs=P("band", None, "ga"), check_vma=False
    )
```

profile of v0, /device:TPU:0, one launch (start us, length us, event | category | flops | bytes accessed | tf_op | source)
XLA Modules:
  0.0 417.0 jit_solution(8911082358564989493)
XLA Ops:
  6.5 11.4 %copy.45 = bf16[64,2,8192]{0,1,2:T(2,128)(2,1)} copy(bf16[64,2,8192]{2,1,0:T(2,128)(2,1)} %param.5) | data formatting | bytes 4194304 | tf_op args[0]
  17.9 7.5 %reshape.39 = bf16[16,2,32768]{2,1,0:T(2,128)(2,1)} reshape(bf16[8192,2,64]{2,1,0:T(2,128)(2,1)} %bitcast.46) | data formatting | bytes 4194304
  25.4 0.0 copy-start
  25.4 8.5 %all-to-all-start = ((bf16[16,2,32768]{2,1,0:T(2,128)(2,1)}), bf16[16,2,32768]{2,1,0:T(2,128)(2,1)}, u32[]{:S(2)}, u32[]{:S(2)}) async-start(bf16[16,2,32768]{2,1,0:T(2,128)(2,1)} %reshape.39), calls=%async_computation | async-start | bytes 4194304 | tf_op jit(solution)/shard_map/all_to_all | solution.py:62
  34.0 0.0 all-reduce.2.cloned.1.call-start
  34.0 0.0 copy-done
  34.0 0.5 copy.60
  34.5 42.6 %all-to-all-done = bf16[16,2,32768]{2,1,0:T(2,128)(2,1)} async-done(((bf16[16,2,32768]{2,1,0:T(2,128)(2,1)}), bf16[16,2,32768]{2,1,0:T(2,128)(2,1)}, u32[]{:S(2)}, u32[]{:S(2)}) %all-to-all-start) | async-done | bytes 2097184 | tf_op jit(solution)/shard_map/all_to_all | solution.py:62
  77.1 7.4 %reshape.40 = bf16[8192,2,64]{2,1,0:T(2,128)(2,1)} reshape(bf16[16,2,32768]{2,1,0:T(2,128)(2,1)} %all-to-all-done) | data formatting | bytes 4194304
  84.4 10.6 %copy.55 = bf16[64,2,16,512]{3,0,2,1:T(8,128)(2,1)} copy(bf16[64,2,16,512]{0,1,3,2:T(2,128)(2,1)} %bitcast.44) | data formatting | bytes 4194304 | tf_op jit(solution)/shard_map/all_to_all | solution.py:62
  95.0 7.4 %copy.54 = bf16[64,2,16,512]{3,2,0,1:T(8,128)(2,1)} copy(bf16[64,2,16,512]{0,1,3,2:T(2,128)(2,1)} %bitcast.45) | data formatting | bytes 4194304 | tf_op jit(solution)/shard_map/all_to_all | solution.py:62
  102.4 0.0 copy-start.1
  102.4 1.8 slice_bitcast_fusion
  104.2 0.4 copy-done.1
  104.6 2.2 copy.47
  106.8 0.6 copy.59
  107.4 12.5 %fusion.6 = f32[864,2048]{1,0:T(8,128)} fusion(bf16[864,1024]{1,0:T(8,128)(2,1)S(1)} %bitcast.53, bf16[1024,512]{1,0:T(8,128)(2,1)S(1)} %get-tuple-element.8, bf16[1024,512]{1,0:T(8,128)(2,1)S(1)} %get-tuple-element.7, bf16[1024,1024]{1,0:T(8,128)(2,1)S(1)} %bitcast.52), kind=kOutput, calls=%fused_computation.6 | convolution fusion | flops 3636461568 | bytes 13041664 | tf_op jit(solution)/shard_map/dot_general | solution.py:39
  119.9 7.9 %reshape.36 = f32[48,18,2048]{2,1,0:T(8,128)} reshape(f32[864,2048]{1,0:T(8,128)} %fusion.6) | data formatting | bytes 14155776 | tf_op jit(solution)/shard_map/reshape | solution.py:28
  127.8 0.0 copy-start.5
  127.8 0.0 copy-start.6
  127.8 0.0 copy-start.7
  127.8 0.0 all-reduce.2.cloned.1.call-update
  127.8 0.7 copy-done.5
  128.6 0.1 reshape.32
  128.6 0.1 dot_general.22
  128.8 0.0 copy-done.6
  128.8 0.0 copy-done.7
  128.8 0.2 select_reduce_fusion
  128.9 0.4 fusion.16
  129.4 0.3 copy.49
  129.7 4.2 %fusion.22 = (bf16[864,1,512]{2,1,0:T(2,128)(2,1)}, bf16[864,1,512]{2,1,0:T(2,128)(2,1)}) fusion(bf16[864,2,512]{2,1,0:T(2,128)(2,1)S(1)} %copy-done), kind=kLoop, calls=%fused_computation.30 | loop fusion | bytes 3538944 | tf_op jit(solution)/shard_map/slice | solution.py:53
  133.9 189.5 %all-reduce.2.cloned.1.call-done = f32[48,18,2048]{2,1,0:T(8,128)} async-done(((f32[48,18,2048]{2,1,0:T(8,128)}), f32[48,18,2048]{2,1,0:T(8,128)}) %all-reduce.2.cloned.1.call-update) | async-done | bytes 7077904 | tf_op jit(solution)/shard_map/psum | solution.py:64
  323.4 12.2 %convolution_convert_fusion = bf16[48,18,2048]{2,1,0:T(8,128)(2,1)} fusion(f32[48,18,18]{2,1,0:T(8,128)S(1)} %copy.49, f32[48,18,2048]{2,1,0:T(8,128)} %all-reduce.2.cloned.1.call-done), kind=kOutput, calls=%fused_computation.7 | convolution fusion | flops 383975424 | bytes 10679040 | tf_op jit(solution)/shard_map/aij,ajc->aic/dot_general | solution.py:29
  335.5 0.0 copy-start.4
  335.5 6.2 %convert_element_type.12 = bf16[864,2048]{1,0:T(8,128)(2,1)} reshape(bf16[48,18,2048]{2,1,0:T(8,128)(2,1)} %convolution_convert_fusion) | data formatting | bytes 7077888 | tf_op jit(solution)/shard_map/convert_element_type | solution.py:30
  341.7 0.0 copy-done.4
  341.7 0.0 copy-start.2
  341.7 0.0 copy-start.3
  341.8 4.6 %fusion.14 = f32[2048,512]{1,0:T(8,128)S(1)} fusion(bf16[864,2048]{1,0:T(8,128)(2,1)} %convert_element_type.12, bf16[864,1,512]{2,1,0:T(2,128)(2,1)S(1)} %copy-done.4), kind=kOutput, calls=%fused_computation.19 | convolution fusion | flops 1811939328 | bytes 8617984 | tf_op jit(solution)/shard_map/dot_general | solution.py:52
  346.3 0.0 copy-done.2
  346.4 0.0 copy-done.3
  346.4 2.4 fusion.15
  348.8 1.2 fusion.11
  350.0 0.2 pad_maximum_fusion
  350.2 2.2 copy.52
  352.4 54.2 %all_to_all.36 = bf16[1024,2,512]{2,1,0:T(2,128)(2,1)S(1)} all-to-all(bf16[1024,2,512]{2,1,0:T(2,128)(2,1)S(1)} %copy.52), channel_id=1, replica_groups=mesh['ga'=2,'band'=16] {'band'}, dimensions={0} | all-to-all | bytes 4194304 | tf_op jit(solution)/shard_map/all_to_all | solution.py:67
  406.5 3.6 copy.58
  (2 shorter events, 0.0 us)
Async XLA Ops:
  25.4 8.6 %copy-start = (bf16[864,2,512]{2,1,0:T(2,128)(2,1)S(1)}, bf16[864,2,512]{2,1,0:T(2,128)(2,1)}, u32[]{:S(2)}) copy-start(bf16[864,2,512]{2,1,0:T(2,128)(2,1)} %param.6) | copy-start | bytes 5308420
  25.4 51.6 %all-to-all-start = ((bf16[16,2,32768]{2,1,0:T(2,128)(2,1)}), bf16[16,2,32768]{2,1,0:T(2,128)(2,1)}, u32[]{:S(2)}, u32[]{:S(2)}) async-start(bf16[16,2,32768]{2,1,0:T(2,128)(2,1)} %reshape.39), calls=%async_computation | async-start | bytes 4194304 | tf_op jit(solution)/shard_map/all_to_all | solution.py:62
  34.0 289.4 %all-reduce.2.cloned.1.call-start = ((), (), s32[]{:S(2)}) async-start(), calls=%async_computation.2 | async-start | bytes 18874368 | tf_op jit(solution)/shard_map/psum | solution.py:64
  102.4 2.2 copy-start.1
  127.8 0.8 copy-start.5
  127.8 1.0 copy-start.6
  127.8 1.0 copy-start.7
  335.5 6.2 %copy-start.4 = (bf16[864,1,512]{2,1,0:T(2,128)(2,1)S(1)}, bf16[864,1,512]{2,1,0:T(2,128)(2,1)}, u32[]{:S(2)}) copy-start(bf16[864,1,512]{2,1,0:T(2,128)(2,1)} %get-tuple-element.9) | copy-start | bytes 2654212
  341.7 4.6 %copy-start.2 = (bf16[864,2048]{1,0:T(8,128)(2,1)S(1)}, bf16[864,2048]{1,0:T(8,128)(2,1)}, u32[]{:S(2)}) copy-start(bf16[864,2048]{1,0:T(8,128)(2,1)} %convert_element_type.12) | copy-start | bytes 10616836
  341.7 4.6 %copy-start.3 = (bf16[864,1,512]{2,1,0:T(2,128)(2,1)S(1)}, bf16[864,1,512]{2,1,0:T(2,128)(2,1)}, u32[]{:S(2)}) copy-start(bf16[864,1,512]{2,1,0:T(2,128)(2,1)} %get-tuple-element.10) | copy-start | bytes 2654212
Sparse Core Ops, SparseCore 0:
  127.9 195.3 all-reduce.1
where the time goes:
time: 419 us; the launch traced here: 417 us
  waiting for transfers between devices  232 us (55%)
  local copies, waits for them, and re-layouts  73.2 us (17%)
  blocking collectives  54.2 us (13%)
  matrix products  32 us (8%)
  between operations  13.6 us (3%)
  starting transfers between devices  8.57 us (2%)
    psum x1, waiting for transfers between devices, per_device(): becp = lax.psum(partial_value, ('ga', 'band'))  189 us
    all_to_all x1, blocking collectives, per_device(): lax.all_to_all(result, 'band', split_axis=0, concat_axis=2, tiled=True)  54.2 us
    all_to_all x1, waiting for transfers between devices, per_device(): lax.all_to_all(orbitals, 'band', split_axis=2, concat_axis=0, tiled=True)  42.6 us
    unnamed x22, local copies, waits for them, and re-layouts  28.5 us
    all_to_all x3, local copies, waits for them, and re-layouts, per_device(): lax.all_to_all(orbitals, 'band', split_axis=2, concat_axis=0, tiled=True)  20.1 us
    dot_general x1, matrix products, project_bands(): lax.dot_general(flat_proj, stacked, (((1,), (1,)), ((), ())), preferred_e...  12.5 us
    dot_general x1, matrix products, apply_coupling(): jnp.einsum('aij,ajc->aic', matrices, blocked, precision=lax.Precision.HIG...  12.2 us
    all_to_all x1, starting transfers between devices, per_device(): lax.all_to_all(orbitals, 'band', split_axis=2, concat_axis=0, tiled=True)  8.52 us
  transfers between devices with their start and end apart: 2, of which 2 were waited for; matrix products, arithmetic and copies ran while one was open for 1% of the time, Pallas kernels for 0%

commit v1 on v0

--- a/solution.py
+++ b/solution.py
@@ -61,7 +61,9 @@
     matrices = block_matrices(coupling, species, offsets)
     spread = lax.all_to_all(orbitals, "band", split_axis=2, concat_axis=0, tiled=True)
     partial_value = project_bands(projectors, spread)
-    becp = lax.psum(partial_value, ("ga", "band"))
+    becp = partial_value
+    for b in ("band", "ga"):
+        becp = lax.psum(becp, axis_name=b)
     dbecp = apply_coupling(matrices, becp)
     result = add_back(projectors, dbecp)
     return lax.all_to_all(result, "band", split_axis=0, concat_axis=2, tiled=True)

time: 419 us -> 510 us (1.22)
  waiting for transfers between devices: 232 us -> 308 us
  local copies, waits for them, and re-layouts: 73.2 us -> 86.9 us
    psum x1 -> x2, waiting for transfers between devices: 189 us -> 265 us  [per_device(): becp = lax.psum(becp, axis_name=b)]
    reshape x0 -> x1, local copies, waits for them, and re-layouts: none -> 10.3 us  [project_bands(): return partial_value.reshape(total_proj, 2, total_bands)]
  transfers between devices with their start and end apart: 2 -> 3, of which waited for: 2 -> 3; matrix products, arithmetic and copies ran while one was open for 1% -> 1% of each run, Pallas kernels for 0% -> 0%
where the time goes in v1:
time: 510 us; the launch traced here: 508 us
  waiting for transfers between devices  308 us (60%)
  local copies, waits for them, and re-layouts  86.9 us (17%)
  blocking collectives  55.8 us (11%)
  matrix products  32 us (6%)
  between operations  13.6 us (3%)
  starting transfers between devices  8.79 us (2%)
    psum x2, waiting for transfers between devices, per_device(): becp = lax.psum(becp, axis_name=b)  265 us
    all_to_all x1, blocking collectives, per_device(): lax.all_to_all(result, 'band', split_axis=0, concat_axis=2, tiled=True)  55.8 us
    all_to_all x1, waiting for transfers between devices, per_device(): lax.all_to_all(orbitals, 'band', split_axis=2, concat_axis=0, tiled=True)  42.6 us
    unnamed x22, local copies, waits for them, and re-layouts  28.5 us
    all_to_all x3, local copies, waits for them, and re-layouts, per_device(): lax.all_to_all(orbitals, 'band', split_axis=2, concat_axis=0, tiled=True)  20.1 us
    dot_general x1, matrix products, project_bands(): lax.dot_general(flat_proj, stacked, (((1,), (1,)), ((), ())), preferred_e...  12.5 us
    dot_general x1, matrix products, apply_coupling(): jnp.einsum('aij,ajc->aic', matrices, blocked, precision=lax.Precision.HIG...  12.2 us
    reshape x1, local copies, waits for them, and re-layouts, apply_coupling(): blocked = becp.reshape(count, per_atom, 2 * widths)  10.9 us
  transfers between devices with their start and end apart: 3, of which 3 were waited for; matrix products, arithmetic and copies ran while one was open for 1% of the time, Pallas kernels for 0%

profile of v1, /device:TPU:0, one launch (start us, length us, event | category | flops | bytes accessed | tf_op | source)
XLA Modules:
  0.0 508.1 jit_solution(11888097500540679888)
XLA Ops:
  6.5 11.4 %copy.45 = bf16[64,2,8192]{0,1,2:T(2,128)(2,1)} copy(bf16[64,2,8192]{2,1,0:T(2,128)(2,1)} %param.5) | data formatting | bytes 4194304 | tf_op args[0]
  17.9 7.5 %reshape.38 = bf16[16,2,32768]{2,1,0:T(2,128)(2,1)} reshape(bf16[8192,2,64]{2,1,0:T(2,128)(2,1)} %bitcast.46) | data formatting | bytes 4194304
  25.4 0.0 copy-start
  25.4 8.5 %all-to-all-start = ((bf16[16,2,32768]{2,1,0:T(2,128)(2,1)}), bf16[16,2,32768]{2,1,0:T(2,128)(2,1)}, u32[]{:S(2)}, u32[]{:S(2)}) async-start(bf16[16,2,32768]{2,1,0:T(2,128)(2,1)} %reshape.38), calls=%async_computation | async-start | bytes 4194304 | tf_op jit(solution)/shard_map/all_to_all | solution.py:62
  34.0 0.0 all-reduce.3.cloned.1.call-start
  34.0 0.0 copy-done
  34.0 0.5 copy.60
  34.5 42.6 %all-to-all-done = bf16[16,2,32768]{2,1,0:T(2,128)(2,1)} async-done(((bf16[16,2,32768]{2,1,0:T(2,128)(2,1)}), bf16[16,2,32768]{2,1,0:T(2,128)(2,1)}, u32[]{:S(2)}, u32[]{:S(2)}) %all-to-all-start) | async-done | bytes 2097184 | tf_op jit(solution)/shard_map/all_to_all | solution.py:62
  77.1 7.4 %reshape.39 = bf16[8192,2,64]{2,1,0:T(2,128)(2,1)} reshape(bf16[16,2,32768]{2,1,0:T(2,128)(2,1)} %all-to-all-done) | data formatting | bytes 4194304
  84.4 10.6 %copy.55 = bf16[64,2,16,512]{3,0,2,1:T(8,128)(2,1)} copy(bf16[64,2,16,512]{0,1,3,2:T(2,128)(2,1)} %bitcast.44) | data formatting | bytes 4194304 | tf_op jit(solution)/shard_map/all_to_all | solution.py:62
  95.0 7.4 %copy.54 = bf16[64,2,16,512]{3,2,0,1:T(8,128)(2,1)} copy(bf16[64,2,16,512]{0,1,3,2:T(2,128)(2,1)} %bitcast.45) | data formatting | bytes 4194304 | tf_op jit(solution)/shard_map/all_to_all | solution.py:62
  102.4 0.0 copy-start.1
  102.4 1.8 slice_bitcast_fusion
  104.2 0.4 copy-done.1
  104.6 2.2 copy.47
  106.8 0.6 copy.59
  107.4 12.5 %fusion.6 = f32[864,2048]{1,0:T(8,128)} fusion(bf16[864,1024]{1,0:T(8,128)(2,1)S(1)} %bitcast.53, bf16[1024,512]{1,0:T(8,128)(2,1)S(1)} %get-tuple-element.8, bf16[1024,512]{1,0:T(8,128)(2,1)S(1)} %get-tuple-element.7, bf16[1024,1024]{1,0:T(8,128)(2,1)S(1)} %bitcast.52), kind=kOutput, calls=%fused_computation.6 | convolution fusion | flops 3636461568 | bytes 13041664 | tf_op jit(solution)/shard_map/dot_general | solution.py:39
  119.9 10.3 %reshape.35 = f32[864,2,1024]{2,1,0:T(2,128)} reshape(f32[864,2048]{1,0:T(8,128)} %fusion.6) | data formatting | bytes 14155776 | tf_op jit(solution)/shard_map/reshape | solution.py:42
  130.2 0.0 all-reduce.3.cloned.1.call-update
  130.2 0.2 all-reduce.5.cloned.1.call-start
  130.5 231.1 %all-reduce.3.cloned.1.call-done = f32[864,2,1024]{2,1,0:T(2,128)} async-done(((f32[864,2,1024]{2,1,0:T(2,128)}), f32[864,2,1024]{2,1,0:T(2,128)}) %all-reduce.3.cloned.1.call-update) | async-done | bytes 7077904 | tf_op jit(solution)/shard_map/psum | solution.py:66
  361.6 10.9 %reshape.36 = f32[48,18,2048]{2,1,0:T(8,128)} reshape(f32[864,2,1024]{2,1,0:T(2,128)} %all-reduce.3.cloned.1.call-done) | data formatting | bytes 14155776 | tf_op jit(solution)/shard_map/reshape | solution.py:28
  372.5 0.0 copy-start.5
  372.5 0.0 copy-start.6
  372.5 0.0 copy-start.7
  372.5 0.0 all-reduce.5.cloned.1.call-update
  372.5 0.7 copy-done.5
  373.3 0.1 reshape.32
  373.4 0.1 dot_general.22
  373.5 0.0 copy-done.6
  373.5 0.0 copy-done.7
  373.5 0.2 select_reduce_fusion
  373.7 0.4 fusion.16
  374.1 0.3 copy.49
  374.4 4.5 fusion.22
  378.9 33.9 %all-reduce.5.cloned.1.call-done = f32[48,18,2048]{2,1,0:T(8,128)} async-done(((f32[48,18,2048]{2,1,0:T(8,128)}), f32[48,18,2048]{2,1,0:T(8,128)}) %all-reduce.5.cloned.1.call-update) | async-done | bytes 7077904 | tf_op jit(solution)/shard_map/psum | solution.py:66
  412.8 12.2 %convolution_convert_fusion = bf16[48,18,2048]{2,1,0:T(8,128)(2,1)} fusion(f32[48,18,18]{2,1,0:T(8,128)S(1)} %copy.49, f32[48,18,2048]{2,1,0:T(8,128)} %all-reduce.5.cloned.1.call-done), kind=kOutput, calls=%fused_computation.7 | convolution fusion | flops 383975424 | bytes 10679040 | tf_op jit(solution)/shard_map/aij,ajc->aic/dot_general | solution.py:29
  425.0 6.2 %convert_element_type.12 = bf16[864,2048]{1,0:T(8,128)(2,1)} reshape(bf16[48,18,2048]{2,1,0:T(8,128)(2,1)} %convolution_convert_fusion) | data formatting | bytes 7077888 | tf_op jit(solution)/shard_map/convert_element_type | solution.py:30
  431.2 0.0 copy-done.4
  431.2 4.6 fusion.14
  435.8 0.0 copy-done.2
  435.8 0.0 copy-done.3
  435.8 2.4 fusion.15
  438.2 1.2 fusion.11
  439.5 0.2 pad_maximum_fusion
  439.7 2.2 copy.52
  441.8 55.8 %all_to_all.36 = bf16[1024,2,512]{2,1,0:T(2,128)(2,1)S(1)} all-to-all(bf16[1024,2,512]{2,1,0:T(2,128)(2,1)S(1)} %copy.52), channel_id=1, replica_groups=mesh['ga'=2,'band'=16] {'band'}, dimensions={0} | all-to-all | bytes 4194304 | tf_op jit(solution)/shard_map/all_to_all | solution.py:69
  497.6 3.6 copy.58
  (5 shorter events, 0.0 us)
Async XLA Ops:
  25.4 8.6 %copy-start = (bf16[864,2,512]{2,1,0:T(2,128)(2,1)S(1)}, bf16[864,2,512]{2,1,0:T(2,128)(2,1)}, u32[]{:S(2)}) copy-start(bf16[864,2,512]{2,1,0:T(2,128)(2,1)} %param.6) | copy-start | bytes 5308420
  25.4 51.6 %all-to-all-start = ((bf16[16,2,32768]{2,1,0:T(2,128)(2,1)}), bf16[16,2,32768]{2,1,0:T(2,128)(2,1)}, u32[]{:S(2)}, u32[]{:S(2)}) async-start(bf16[16,2,32768]{2,1,0:T(2,128)(2,1)} %reshape.38), calls=%async_computation | async-start | bytes 4194304 | tf_op jit(solution)/shard_map/all_to_all | solution.py:62
  34.0 327.6 %all-reduce.3.cloned.1.call-start = ((), (), s32[]{:S(2)}) async-start(), calls=%async_computation.2 | async-start | bytes 14155776 | tf_op jit(solution)/shard_map/psum | solution.py:66
  102.4 2.2 copy-start.1
  130.2 282.6 %all-reduce.5.cloned.1.call-start = ((), (), s32[]{:S(2)}) async-start(), calls=%async_computation.3 | async-start | bytes 18874368 | tf_op jit(solution)/shard_map/psum | solution.py:66
  372.5 0.8 copy-start.5
  372.5 1.0 copy-start.6
  372.5 1.0 copy-start.7
  425.0 6.2 %copy-start.4 = (bf16[864,1,512]{2,1,0:T(2,128)(2,1)S(1)}, bf16[864,1,512]{2,1,0:T(2,128)(2,1)}, u32[]{:S(2)}) copy-start(bf16[864,1,512]{2,1,0:T(2,128)(2,1)} %get-tuple-element.9) | copy-start | bytes 2654212
  431.2 4.6 copy-start.2
  431.2 4.6 copy-start.3
Sparse Core Ops, SparseCore 0:
  130.4 231.1 all-reduce.2
  372.7 40.1 all-reduce.4
